TPU v7x, 32 devices: a whole 2x2x4 slice. The times are simulated.
32 devices in a mesh: grp: 4 (over z), sp: 8 (over y, x, core).
Axes of the slice: x: 2, y: 2, z: 4, core: 2. Of those that a mesh axis runs over, the one named last changes fastest.
Arguments:
- tokens: bfloat16 [2048, 2880], P(('grp', 'sp')), may hold values from -36 to 36
- query_weight: bfloat16 [2880, 2048], P(None, 'sp'), may hold values from -0.109375 to 0.109375
- key_value_weight: bfloat16 [2880, 1024], replicated, may hold values from -0.109375 to 0.109375
- block_places: int32 [16], replicated, may hold values from 0 to 15, each once
- sinks: float32 [32], replicated, may hold values from -1 to 5
Outputs:
- attended: bfloat16 [2048, 2048], P(('grp', 'sp'))
Inputs may be any that keep to these rules, and one draw needn't show every extreme that they name: `block_places`: every sequence block appears once.
All inputs are finite; a program needn't handle non-finite values.
Results may differ from a plain program's by a relative error of at most 0.008.
The roundings to bfloat16 on the way count: a program that leaves them out, or rounds other values in their place, can miss the bound.
Values may be sent and summed in bfloat16 or wider, within the bound.
A program may use at most 128 MiB of HBM per device.

v0:
```python
import jax
import jax.numpy as jnp
from jax import lax
from jax.sharding import PartitionSpec as P

QUERY_HEADS = 32
HEAD_SIZE = 64
BPG = 4
rope_base = 150000.0
neg_large = -1e30


def rotate(vectors, angles):
    middle = vectors.shape[-1] // 2
    first_half = vectors[..., :middle]
    second_half = vectors[..., middle:]
    cosine = jnp.cos(angles)
    sine_part = jnp.sin(angles)
    return jnp.concatenate(
        [
            first_half * cosine - second_half * sine_part,
            second_half * cosine + first_half * sine_part,
        ],
        axis=-1,
    )


def locate(stored, block_rows, block_places):
    blocks = stored // block_rows
    table = jnp.arange(block_places.shape[0], dtype=jnp.int32)
    onehot = (blocks[:, None] == table[None, :]).astype(jnp.int32)
    return jnp.sum(onehot * block_places[None, :], axis=1) * block_rows + stored % block_rows


def prepare(projected, own_places, query_cols, kv_cols, head_count):
    row_count = projected.shape[0]
    inverse = rope_base ** (-(jnp.arange(HEAD_SIZE // 2, dtype=jnp.float32) * 2.0) / HEAD_SIZE)
    angles = own_places.astype(jnp.float32)[:, None, None] * inverse[None, None, :]
    queries = rotate(
        projected[:, :query_cols].reshape(row_count, query_cols // HEAD_SIZE, HEAD_SIZE), angles
    ).astype(jnp.bfloat16)
    rotated_keys = rotate(
        projected[:, query_cols : query_cols + kv_cols].reshape(row_count, head_count, HEAD_SIZE),
        angles,
    )
    key_value_pair = jnp.concatenate(
        [rotated_keys.reshape(row_count, kv_cols), projected[:, query_cols + kv_cols :]], axis=1
    ).astype(jnp.bfloat16)
    return (queries, key_value_pair)


def attend(state, queries, query_places, key_value_pair, key_places, head_count):
    maxima, totals, mixture = state
    key_count = key_value_pair.shape[0]
    column_half = key_value_pair.shape[1] // 2
    key_part = key_value_pair[:, :column_half].reshape(key_count, head_count, HEAD_SIZE)
    value_part = key_value_pair[:, column_half:].reshape(key_count, head_count, HEAD_SIZE)
    scores = jnp.einsum(
        "qhgd,khd->hgqk", queries, key_part, preferred_element_type=jnp.float32
    ) * HEAD_SIZE ** (-0.5)
    allowed = key_places[None, :] <= query_places[:, None]
    scores = jnp.where(allowed, scores, neg_large)
    updated = jnp.maximum(maxima, jnp.max(scores, axis=-1))
    weights = jnp.where(allowed, jnp.exp(scores - updated[..., None]), 0.0)
    factor = jnp.exp(maxima - updated)
    totals = totals * factor + jnp.sum(weights, axis=-1)
    mixture = mixture * factor[..., None] + jnp.einsum(
        "hgqk,khd->hgqd",
        weights.astype(jnp.bfloat16),
        value_part,
        preferred_element_type=jnp.float32,
    )
    return (updated, totals, mixture)


def per_device(tokens, query_weight, key_value_weight, block_places, sinks):
    sp_count = lax.axis_size("sp")
    local_rows = tokens.shape[0]
    group_rows = local_rows * sp_count
    block_rows = group_rows // BPG
    kv_total = key_value_weight.shape[1] // (2 * HEAD_SIZE)
    sp_place = lax.axis_index("sp")
    grp_place = lax.axis_index("grp")
    query_cols = query_weight.shape[1]
    query_heads = query_cols // HEAD_SIZE
    head_count = max(kv_total // sp_count, 1)
    kv_cols = head_count * HEAD_SIZE
    first_head = sp_place * query_heads // (QUERY_HEADS // kv_total)
    key_weight = lax.dynamic_slice_in_dim(key_value_weight, first_head * HEAD_SIZE, kv_cols, 1)
    value_weight = lax.dynamic_slice_in_dim(
        key_value_weight, kv_total * HEAD_SIZE + first_head * HEAD_SIZE, kv_cols, 1
    )
    joined = jnp.concatenate([query_weight, key_weight, value_weight], axis=1)
    projected = jnp.dot(
        lax.all_gather(tokens, "sp", axis=0, tiled=True), joined, preferred_element_type=jnp.float32
    )
    query_local = jnp.arange(group_rows, dtype=jnp.int32)
    head_first = sp_place * query_heads
    own_places = locate(grp_place * group_rows + query_local, block_rows, block_places)
    queries, key_value_pair = prepare(projected, own_places, query_cols, kv_cols, head_count)
    query_sharing = query_heads // head_count
    head_sinks = lax.dynamic_slice_in_dim(sinks, head_first, query_heads, 0).reshape(
        head_count, query_sharing
    )
    sink_rows = jnp.broadcast_to(head_sinks[:, :, None], (head_count, query_sharing, group_rows))
    query_block4 = queries.reshape(group_rows, head_count, query_sharing, HEAD_SIZE)
    initial = (
        sink_rows,
        jnp.ones((head_count, query_sharing, group_rows), jnp.float32),
        jnp.zeros((head_count, query_sharing, group_rows, HEAD_SIZE), jnp.float32),
    )
    piece = lax.all_gather(key_value_pair, "grp", axis=0, tiled=True)
    step_rows = min(piece.shape[0], group_rows)
    turns = piece.shape[0] // step_rows

    def visit(turn, inner):
        offset = turn * step_rows
        piece_rows = lax.dynamic_slice_in_dim(piece, offset, step_rows, 0)
        position = offset + jnp.arange(step_rows, dtype=jnp.int32)
        stored = position // group_rows * group_rows + position % group_rows
        key_places = locate(stored, block_rows, block_places)
        return attend(inner, query_block4, own_places, piece_rows, key_places, head_count)

    maxima, totals, mixture = lax.fori_loop(0, turns, visit, initial)
    normed = jnp.transpose(mixture, (2, 0, 1, 3)) / jnp.transpose(totals, (2, 0, 1))[..., None]
    attended = normed.reshape(group_rows, query_cols).astype(jnp.bfloat16)
    return lax.all_to_all(attended, "sp", split_axis=0, concat_axis=1, tiled=True)


def solution(mesh):
    in_specs = (P(("grp", "sp"), None), P(None, "sp"), P(), P(), P())
    out_specs = P(("grp", "sp"), None)
    return jax.shard_map(
        per_device, mesh=mesh, in_specs=in_specs, out_specs=out_specs, check_vma=False
    )
```

profile of v0, /device:TPU:0, one launch (start us, length us, event | category | flops | bytes accessed | tf_op | source)
XLA Modules:
  0.0 114.0 jit_solution(16821734951300925589)
XLA Ops:
  6.5 0.0 all-gather.2.cloned.1.call-start
  6.5 0.7 all-gather.2.cloned.1.call-update
  7.3 0.7 dynamic_slice.20
  8.1 0.7 select_reduce_fusion.1
  8.8 0.3 multiply_cosine_fusion
  9.1 1.8 %constant_dynamic-slice_fusion.1 = (bf16[2880,64]{1,0:T(8,128)(2,1)S(1)}, bf16[2880,64]{1,0:T(8,128)(2,1)S(1)}) fusion(bf16[2880,1024]{1,0:T(8,128)(2,1)} %param.9, s32[]{:T(128)S(6)} %select_n.163, s32[]{:T(128)S(6)} %select_n.164), kind=kLoop, calls=%fused_computation.92 | loop fusion | bytes 1474568 | tf_op jit(solution)/shard_map/dynamic_slice | solution.py:89
  11.0 32.6 %all-gather.2.cloned.1.call-done = bf16[512,2880]{1,0:T(8,128)(2,1)} async-done(((bf16[64,2880]{1,0:T(8,128)(2,1)}), bf16[512,2880]{1,0:T(8,128)(2,1)}) %all-gather.2.cloned.1.call-update) | async-done | bytes 2949136 | tf_op jit(solution)/shard_map/all_gather | solution.py:95
  43.6 0.0 copy-start.1
  43.6 4.1 %fusion.32 = f32[512,384]{0,1:T(8,128)S(1)} fusion(bf16[512,2880]{1,0:T(8,128)(2,1)} %all-gather.2.cloned.1.call-done, bf16[2880,64]{1,0:T(8,128)(2,1)S(1)} %get-tuple-element.296, bf16[2880,64]{1,0:T(8,128)(2,1)S(1)} %get-tuple-element.295, bf16[2880,256]{1,0:T(8,128)(2,1)} %param.8), kind=kOutput, calls=%fused_computation.53 | convolution fusion | flops 1139097600 | bytes 5947392 | tf_op jit(solution)/shard_map/dot_general | solution.py:94
  47.8 0.3 fusion.43
  48.2 16.0 %all_gather.7 = bf16[2048,128]{0,1:T(8,128)(2,1)S(1)} all-gather(bf16[512,128]{0,1:T(8,128)(2,1)S(1)} %pad_maximum_fusion.1), channel_id=1, replica_groups=mesh['grp'=4,'sp'=8] {'grp'}, dimensions={0}, use_global_device_ids=true | all-gather | bytes 655360 | tf_op jit(solution)/shard_map/all_gather | solution.py:112
  64.2 0.1 fusion.36
  64.3 0.1 broadcast_in_dim.74
  64.4 0.0 copy-done.1
  64.4 31.9 %while.21 = (s32[]{:T(128)}, f32[1,4,512]{2,1,0:T(4,128)S(1)}, f32[1,4,512]{2,1,0:T(4,128)S(1)}, f32[1,4,512,64]{2,3,1,0:T(8,128)S(1)}, s32[16]{0:T(128)S(1)}, /...) while((s32[]{:T(128)}, f32[1,4,512]{2,1,0:T(4,128)S(1)}, ...), condition=%wide.region_5.6_spmd.clone, body=%wide.region_1.5_spmd.clone.sunk | while | flops 282791424 | bytes 31996208 | solution.py:124
  64.4 0.1 select_reduce_fusion.3
  64.5 0.2 broadcast_compare_fusion.3
  64.7 2.8 %fusion.62 = (f32[4,512]{1,0:T(4,128)S(1)}, f32[512,512,4]{1,0,2:T(8,128)}) fusion(pred[512,512]{0,1:T(8,128)(4,1)S(1)} %broadcast_compare_fusion.3, bf16[512,1,4,64]{0,3,2,1:T(8,128)(2,1)S(1)} %get-tuple-element.393, bf16[2048,128]{0,1:T(8,128)(2,1)S(1)} %get-tuple-element.392, s32[]{:T(128)S(6)} %select_n.256), kind=kOutput, calls=%fused_computation.2.clone.1 | convolution fusion | flops 137361408 | bytes 4792324 | tf_op jit(solution)/shard_map/while/body/eval_jaxpr/qhgd,khd->hgqk/dot_general | solution.py:58
  67.5 0.0 copy-start
  67.6 3.7 %fusion.65 = f32[1,4,512,64]{2,3,1,0:T(8,128)S(1)} fusion(f32[512,512,4]{1,0,2:T(8,128)} %get-tuple-element.358, f32[4,512]{1,0:T(4,128)S(1)} %bitcast.99, pred[512,512]{0,1:T(8,128)(4,1)S(1)} %broadcast_compare_fusion.3, f32[1,4,512,64]{2,3,1,0:T(8,128)S(1)} %get-tuple-element.376, f32[4,512]{1,0:T(4,128)S(1)} %get-tuple-element.359, ...), kind=kOutput, calls=%fused_computation.9.clone.1 | convolution fusion | flops 139853824 | bytes 5586953 | tf_op jit(solution)/shard_map/while/body/eval_jaxpr/hgqk,khd->hgqd/dot_general | solution.py:67
  71.3 0.0 copy-done
  71.3 1.0 fusion.64
  72.4 0.1 select_reduce_fusion.3
  72.5 0.2 broadcast_compare_fusion.3
  72.7 2.8 %fusion.62 = (f32[4,512]{1,0:T(4,128)S(1)}, f32[512,512,4]{1,0,2:T(8,128)}) fusion(pred[512,512]{0,1:T(8,128)(4,1)S(1)} %broadcast_compare_fusion.3, bf16[512,1,4,64]{0,3,2,1:T(8,128)(2,1)S(1)} %get-tuple-element.393, bf16[2048,128]{0,1:T(8,128)(2,1)S(1)} %get-tuple-element.392, s32[]{:T(128)S(6)} %select_n.256), kind=kOutput, calls=%fused_computation.2.clone.1 | convolution fusion | flops 137361408 | bytes 4792324 | tf_op jit(solution)/shard_map/while/body/eval_jaxpr/qhgd,khd->hgqk/dot_general | solution.py:58
  75.5 0.0 copy-start
  75.6 3.7 %fusion.65 = f32[1,4,512,64]{2,3,1,0:T(8,128)S(1)} fusion(f32[512,512,4]{1,0,2:T(8,128)} %get-tuple-element.358, f32[4,512]{1,0:T(4,128)S(1)} %bitcast.99, pred[512,512]{0,1:T(8,128)(4,1)S(1)} %broadcast_compare_fusion.3, f32[1,4,512,64]{2,3,1,0:T(8,128)S(1)} %get-tuple-element.376, f32[4,512]{1,0:T(4,128)S(1)} %get-tuple-element.359, ...), kind=kOutput, calls=%fused_computation.9.clone.1 | convolution fusion | flops 139853824 | bytes 5586953 | tf_op jit(solution)/shard_map/while/body/eval_jaxpr/hgqk,khd->hgqd/dot_general | solution.py:67
  79.3 0.0 copy-done
  79.3 1.0 fusion.64
  80.4 0.1 select_reduce_fusion.3
  80.5 0.2 broadcast_compare_fusion.3
  80.7 2.8 %fusion.62 = (f32[4,512]{1,0:T(4,128)S(1)}, f32[512,512,4]{1,0,2:T(8,128)}) fusion(pred[512,512]{0,1:T(8,128)(4,1)S(1)} %broadcast_compare_fusion.3, bf16[512,1,4,64]{0,3,2,1:T(8,128)(2,1)S(1)} %get-tuple-element.393, bf16[2048,128]{0,1:T(8,128)(2,1)S(1)} %get-tuple-element.392, s32[]{:T(128)S(6)} %select_n.256), kind=kOutput, calls=%fused_computation.2.clone.1 | convolution fusion | flops 137361408 | bytes 4792324 | tf_op jit(solution)/shard_map/while/body/eval_jaxpr/qhgd,khd->hgqk/dot_general | solution.py:58
  83.5 0.0 copy-start
  83.5 3.7 %fusion.65 = f32[1,4,512,64]{2,3,1,0:T(8,128)S(1)} fusion(f32[512,512,4]{1,0,2:T(8,128)} %get-tuple-element.358, f32[4,512]{1,0:T(4,128)S(1)} %bitcast.99, pred[512,512]{0,1:T(8,128)(4,1)S(1)} %broadcast_compare_fusion.3, f32[1,4,512,64]{2,3,1,0:T(8,128)S(1)} %get-tuple-element.376, f32[4,512]{1,0:T(4,128)S(1)} %get-tuple-element.359, ...), kind=kOutput, calls=%fused_computation.9.clone.1 | convolution fusion | flops 139853824 | bytes 5586953 | tf_op jit(solution)/shard_map/while/body/eval_jaxpr/hgqk,khd->hgqd/dot_general | solution.py:67
  87.2 0.0 copy-done
  87.3 1.0 fusion.64
  88.4 0.1 select_reduce_fusion.3
  88.5 0.2 broadcast_compare_fusion.3
  88.7 2.8 %fusion.62 = (f32[4,512]{1,0:T(4,128)S(1)}, f32[512,512,4]{1,0,2:T(8,128)}) fusion(pred[512,512]{0,1:T(8,128)(4,1)S(1)} %broadcast_compare_fusion.3, bf16[512,1,4,64]{0,3,2,1:T(8,128)(2,1)S(1)} %get-tuple-element.393, bf16[2048,128]{0,1:T(8,128)(2,1)S(1)} %get-tuple-element.392, s32[]{:T(128)S(6)} %select_n.256), kind=kOutput, calls=%fused_computation.2.clone.1 | convolution fusion | flops 137361408 | bytes 4792324 | tf_op jit(solution)/shard_map/while/body/eval_jaxpr/qhgd,khd->hgqk/dot_general | solution.py:58
  91.5 0.0 copy-start
  91.5 3.7 %fusion.65 = f32[1,4,512,64]{2,3,1,0:T(8,128)S(1)} fusion(f32[512,512,4]{1,0,2:T(8,128)} %get-tuple-element.358, f32[4,512]{1,0:T(4,128)S(1)} %bitcast.99, pred[512,512]{0,1:T(8,128)(4,1)S(1)} %broadcast_compare_fusion.3, f32[1,4,512,64]{2,3,1,0:T(8,128)S(1)} %get-tuple-element.376, f32[4,512]{1,0:T(4,128)S(1)} %get-tuple-element.359, ...), kind=kOutput, calls=%fused_computation.9.clone.1 | convolution fusion | flops 139853824 | bytes 5586953 | tf_op jit(solution)/shard_map/while/body/eval_jaxpr/hgqk,khd->hgqd/dot_general | solution.py:67
  95.2 0.0 copy-done
  95.3 1.0 fusion.64
  96.3 0.1 fusion.35
  96.4 0.3 convert_element_type.40
  96.7 0.3 copy.15
  97.0 9.4 %all_to_all.16 = bf16[8,64,256]{2,1,0:T(8,128)(2,1)S(1)} all-to-all(bf16[8,64,256]{2,1,0:T(8,128)(2,1)S(1)} %copy.15), channel_id=1, replica_groups=mesh['grp'=4,'sp'=8] {'sp'}, dimensions={0} | all-to-all | bytes 524288 | tf_op jit(solution)/shard_map/all_to_all | solution.py:127
  106.5 0.7 copy.18
  (31 shorter events, 0.4 us)
Async XLA Ops:
  6.5 37.1 %all-gather.2.cloned.1.call-start = ((), (), s32[]{:S(2)}) async-start(), calls=%async_computation.1 | async-start | bytes 3391488 | tf_op jit(solution)/shard_map/all_gather | solution.py:95
  43.6 20.8 %copy-start.1 = (s32[16]{0:T(128)S(1)}, s32[16]{0:T(128)}, u32[]{:S(2)}) copy-start(s32[16]{0:T(128)} %param.10) | copy-start | bytes 196
  67.5 3.7 %copy-start = (f32[512,512,4]{1,0,2:T(8,128)S(1)}, f32[512,512,4]{1,0,2:T(8,128)}, u32[]{:S(2)}) copy-start(f32[512,512,4]{1,0,2:T(8,128)} %get-tuple-element.358) | copy-start | bytes 12582916 | tf_op jit(solution)/shard_map/while
  75.5 3.7 %copy-start = (f32[512,512,4]{1,0,2:T(8,128)S(1)}, f32[512,512,4]{1,0,2:T(8,128)}, u32[]{:S(2)}) copy-start(f32[512,512,4]{1,0,2:T(8,128)} %get-tuple-element.358) | copy-start | bytes 12582916 | tf_op jit(solution)/shard_map/while
  83.5 3.7 %copy-start = (f32[512,512,4]{1,0,2:T(8,128)S(1)}, f32[512,512,4]{1,0,2:T(8,128)}, u32[]{:S(2)}) copy-start(f32[512,512,4]{1,0,2:T(8,128)} %get-tuple-element.358) | copy-start | bytes 12582916 | tf_op jit(solution)/shard_map/while
  91.5 3.7 %copy-start = (f32[512,512,4]{1,0,2:T(8,128)S(1)}, f32[512,512,4]{1,0,2:T(8,128)}, u32[]{:S(2)}) copy-start(f32[512,512,4]{1,0,2:T(8,128)} %get-tuple-element.358) | copy-start | bytes 12582916 | tf_op jit(solution)/shard_map/while
Sparse Core Ops, SparseCore 0:
  9.2 34.3 all-gather.1
where the time goes:
time: 114 us
  waiting for transfers between devices  33.3 us (29%)
  matrix products  30.1 us (26%)
  blocking collectives  25.5 us (22%)
  between operations  13.6 us (12%)
  other arithmetic  7.27 us (6%)
  local copies, waits for them, and re-layouts  4.05 us (4%)
    all_gather x1, waiting for transfers between devices, per_device(): lax.all_gather(tokens, 'sp', axis=0, tiled=True)  32.6 us
    all_gather x1, blocking collectives, per_device(): piece = lax.all_gather(key_value_pair, 'grp', axis=0, tiled=True)  16 us
    dot_general x4, matrix products, attend(): jnp.einsum('hgqk,khd->hgqd', weights.astype(jnp.bfloat16), value_part, pr...  14.8 us
    dot_general x4, matrix products, attend(): jnp.einsum('qhgd,khd->hgqk', queries, key_part, preferred_element_type=jn...  11.2 us
    all_to_all x1, blocking collectives, per_device(): lax.all_to_all(attended, 'sp', split_axis=0, concat_axis=1, tiled=True)  9.44 us
    reduce_sum x4, other arithmetic, attend(): totals = totals * factor + jnp.sum(weights, axis=-1)  4.17 us
    dot_general x1, matrix products, per_device(): jnp.dot(lax.all_gather(tokens, 'sp', axis=0, tiled=True), joined, preferr...  4.11 us
  transfers between devices with their start and end apart: 1, of which 1 were waited for; matrix products, arithmetic and copies ran while one was open for 3% of the time, Pallas kernels for 0%

commit v1 on v0

--- a/solution.py
+++ b/solution.py
@@ -109,7 +109,9 @@
         jnp.ones((head_count, query_sharing, group_rows), jnp.float32),
         jnp.zeros((head_count, query_sharing, group_rows, HEAD_SIZE), jnp.float32),
     )
-    piece = lax.all_gather(key_value_pair, "grp", axis=0, tiled=True)
+    piece = jnp.concatenate(
+        lax.all_to_all(jnp.stack([key_value_pair] * lax.axis_size("grp")), "grp", 0, 0), axis=0
+    )
     step_rows = min(piece.shape[0], group_rows)
     turns = piece.shape[0] // step_rows
 

time: 114 us -> 118 us (1.035)
  blocking collectives: 25.5 us -> 9.42 us
  waiting for transfers between devices: 33.3 us -> 48.8 us
  starting transfers between devices: 0.01 us -> 4.6 us
    all_gather x1 -> x0, blocking collectives: 16 us -> none  [per_device(): piece = lax.all_gather(key_value_pair, 'grp', axis=0, tiled=True)]
    all_to_all x0 -> x1, waiting for transfers between devices: none -> 14.3 us  [per_device(): lax.all_to_all(jnp.stack([key_value_pair] * lax.axis_size('grp')), 'grp',...]
    all_to_all x0 -> x1, starting transfers between devices: none -> 4.6 us  [per_device(): lax.all_to_all(jnp.stack([key_value_pair] * lax.axis_size('grp')), 'grp',...]
  transfers between devices with their start and end apart: 1 -> 2, of which waited for: 1 -> 2; matrix products, arithmetic and copies ran while one was open for 3% -> 3% of each run, Pallas kernels for 0% -> 0%
where the time goes in v1:
time: 118 us
  waiting for transfers between devices  48.8 us (41%)
  matrix products  29.8 us (25%)
  between operations  13.5 us (11%)
  blocking collectives  9.42 us (8%)
  other arithmetic  7.26 us (6%)
  starting transfers between devices  4.6 us (4%)
  local copies, waits for them, and re-layouts  4.49 us (4%)
    all_gather x1, waiting for transfers between devices, per_device(): lax.all_gather(tokens, 'sp', axis=0, tiled=True)  33.7 us
    dot_general x4, matrix products, attend(): jnp.einsum('hgqk,khd->hgqd', weights.astype(jnp.bfloat16), value_part, pr...  14.7 us
    all_to_all x1, waiting for transfers between devices, per_device(): lax.all_to_all(jnp.stack([key_value_pair] * lax.axis_size('grp')), 'grp',...  14.3 us
    dot_general x4, matrix products, attend(): jnp.einsum('qhgd,khd->hgqk', queries, key_part, preferred_element_type=jn...  11 us
    all_to_all x1, blocking collectives, per_device(): lax.all_to_all(attended, 'sp', split_axis=0, concat_axis=1, tiled=True)  9.42 us
    all_to_all x1, starting transfers between devices, per_device(): lax.all_to_all(jnp.stack([key_value_pair] * lax.axis_size('grp')), 'grp',...  4.6 us
    reduce_sum x4, other arithmetic, attend(): totals = totals * factor + jnp.sum(weights, axis=-1)  4.16 us
    dot_general x1, matrix products, per_device(): jnp.dot(lax.all_gather(tokens, 'sp', axis=0, tiled=True), joined, preferr...  4.11 us
  transfers between devices with their start and end apart: 2, of which 2 were waited for; matrix products, arithmetic and copies ran while one was open for 3% of the time, Pallas kernels for 0%

profile of v1, /device:TPU:0, one launch (start us, length us, event | category | flops | bytes accessed | tf_op | source)
XLA Modules:
  0.0 118.2 jit_solution(6765056020342586539)
XLA Ops:
  6.5 0.0 all-gather.2.cloned.1.call-start
  6.5 0.7 all-gather.2.cloned.1.call-update
  7.3 0.7 select_reduce_fusion.1
  8.1 1.8 %constant_dynamic-slice_fusion.1 = (bf16[2880,64]{1,0:T(8,128)(2,1)S(1)}, bf16[2880,64]{1,0:T(8,128)(2,1)S(1)}) fusion(bf16[2880,1024]{1,0:T(8,128)(2,1)} %param.9, s32[]{:T(128)S(6)} %select_n.163, s32[]{:T(128)S(6)} %select_n.164), kind=kLoop, calls=%fused_computation.92 | loop fusion | bytes 1474568 | tf_op jit(solution)/shard_map/dynamic_slice | solution.py:89
  9.9 33.7 %all-gather.2.cloned.1.call-done = bf16[512,2880]{1,0:T(8,128)(2,1)} async-done(((bf16[64,2880]{1,0:T(8,128)(2,1)}), bf16[512,2880]{1,0:T(8,128)(2,1)}) %all-gather.2.cloned.1.call-update) | async-done | bytes 2949136 | tf_op jit(solution)/shard_map/all_gather | solution.py:95
  43.6 0.0 copy-start.2
  43.6 4.1 %fusion.32 = f32[512,384]{0,1:T(8,128)S(1)} fusion(bf16[512,2880]{1,0:T(8,128)(2,1)} %all-gather.2.cloned.1.call-done, bf16[2880,64]{1,0:T(8,128)(2,1)S(1)} %get-tuple-element.312, bf16[2880,64]{1,0:T(8,128)(2,1)S(1)} %get-tuple-element.311, bf16[2880,256]{1,0:T(8,128)(2,1)} %param.8), kind=kOutput, calls=%fused_computation.53 | convolution fusion | flops 1139097600 | bytes 5947392 | tf_op jit(solution)/shard_map/dot_general | solution.py:94
  47.7 0.0 copy-start.1
  47.8 0.3 fusion.43
  48.1 0.8 stack.2
  49.0 4.6 %all-to-all-start = ((bf16[4,512,128]{1,2,0:T(8,128)(2,1)}), bf16[4,512,128]{1,2,0:T(8,128)(2,1)S(1)}, u32[]{:S(2)}, u32[]{:S(2)}) async-start(bf16[4,512,128]{1,2,0:T(8,128)(2,1)} %stack.2), calls=%async_computation | async-start | bytes 1048576 | tf_op jit(solution)/shard_map/all_to_all | solution.py:113
  53.6 0.0 copy-done.2
  53.6 0.1 dynamic_slice.20
  53.6 0.3 multiply_cosine_fusion
  54.0 0.1 fusion.36
  54.1 14.3 %all-to-all-done = bf16[4,512,128]{1,2,0:T(8,128)(2,1)S(1)} async-done(((bf16[4,512,128]{1,2,0:T(8,128)(2,1)}), bf16[4,512,128]{1,2,0:T(8,128)(2,1)S(1)}, u32[]{:S(2)}, u32[]{:S(2)}) %all-to-all-start) | async-done | bytes 524320 | tf_op jit(solution)/shard_map/all_to_all | solution.py:113
  68.5 0.3 copy.20
  68.7 0.1 broadcast_in_dim.74
  68.8 0.0 copy-done.1
  68.8 31.7 %while.21 = (s32[]{:T(128)}, f32[1,4,512]{2,1,0:T(4,128)S(1)}, f32[1,4,512]{2,1,0:T(4,128)S(1)}, f32[1,4,512,64]{2,3,1,0:T(8,128)S(1)}, s32[16]{0:T(128)S(1)}, /...) while((s32[]{:T(128)}, f32[1,4,512]{2,1,0:T(4,128)S(1)}, ...), condition=%wide.region_5.6_spmd.clone, body=%wide.region_1.5_spmd.clone.sunk | while | flops 282791424 | bytes 32127280 | solution.py:126
  68.8 0.1 select_reduce_fusion.3
  69.0 0.2 broadcast_compare_fusion.3
  69.2 2.7 %fusion.62 = (f32[4,512]{1,0:T(4,128)S(1)}, f32[512,512,4]{1,0,2:T(8,128)}) fusion(pred[512,512]{0,1:T(8,128)(4,1)S(1)} %broadcast_compare_fusion.3, bf16[512,1,4,64]{0,3,2,1:T(8,128)(2,1)S(1)} %get-tuple-element.409, bf16[2048,128]{1,0:T(8,128)(2,1)S(1)} %get-tuple-element.408, s32[]{:T(128)S(6)} %select_n.256), kind=kOutput, calls=%fused_computation.2.clone.1 | convolution fusion | flops 137361408 | bytes 4857860 | tf_op jit(solution)/shard_map/while/body/eval_jaxpr/qhgd,khd->hgqk/dot_general | solution.py:58
  71.9 0.0 copy-start
  72.0 3.7 %fusion.65 = f32[1,4,512,64]{2,3,1,0:T(8,128)S(1)} fusion(f32[512,512,4]{1,0,2:T(8,128)} %get-tuple-element.374, f32[4,512]{1,0:T(4,128)S(1)} %bitcast.102, pred[512,512]{0,1:T(8,128)(4,1)S(1)} %broadcast_compare_fusion.3, f32[1,4,512,64]{2,3,1,0:T(8,128)S(1)} %get-tuple-element.392, f32[4,512]{1,0:T(4,128)S(1)} %get-tuple-element.375, ...), kind=kOutput, calls=%fused_computation.9.clone.1 | convolution fusion | flops 139853824 | bytes 5652489 | tf_op jit(solution)/shard_map/while/body/eval_jaxpr/hgqk,khd->hgqd/dot_general | solution.py:67
  75.6 0.0 copy-done
  75.6 1.0 fusion.64
  76.8 0.1 select_reduce_fusion.3
  76.9 0.2 broadcast_compare_fusion.3
  77.1 2.7 %fusion.62 = (f32[4,512]{1,0:T(4,128)S(1)}, f32[512,512,4]{1,0,2:T(8,128)}) fusion(pred[512,512]{0,1:T(8,128)(4,1)S(1)} %broadcast_compare_fusion.3, bf16[512,1,4,64]{0,3,2,1:T(8,128)(2,1)S(1)} %get-tuple-element.409, bf16[2048,128]{1,0:T(8,128)(2,1)S(1)} %get-tuple-element.408, s32[]{:T(128)S(6)} %select_n.256), kind=kOutput, calls=%fused_computation.2.clone.1 | convolution fusion | flops 137361408 | bytes 4857860 | tf_op jit(solution)/shard_map/while/body/eval_jaxpr/qhgd,khd->hgqk/dot_general | solution.py:58
  79.9 0.0 copy-start
  79.9 3.7 %fusion.65 = f32[1,4,512,64]{2,3,1,0:T(8,128)S(1)} fusion(f32[512,512,4]{1,0,2:T(8,128)} %get-tuple-element.374, f32[4,512]{1,0:T(4,128)S(1)} %bitcast.102, pred[512,512]{0,1:T(8,128)(4,1)S(1)} %broadcast_compare_fusion.3, f32[1,4,512,64]{2,3,1,0:T(8,128)S(1)} %get-tuple-element.392, f32[4,512]{1,0:T(4,128)S(1)} %get-tuple-element.375, ...), kind=kOutput, calls=%fused_computation.9.clone.1 | convolution fusion | flops 139853824 | bytes 5652489 | tf_op jit(solution)/shard_map/while/body/eval_jaxpr/hgqk,khd->hgqd/dot_general | solution.py:67
  83.6 0.0 copy-done
  83.6 1.0 fusion.64
  84.7 0.1 select_reduce_fusion.3
  84.8 0.2 broadcast_compare_fusion.3
  85.0 2.7 %fusion.62 = (f32[4,512]{1,0:T(4,128)S(1)}, f32[512,512,4]{1,0,2:T(8,128)}) fusion(pred[512,512]{0,1:T(8,128)(4,1)S(1)} %broadcast_compare_fusion.3, bf16[512,1,4,64]{0,3,2,1:T(8,128)(2,1)S(1)} %get-tuple-element.409, bf16[2048,128]{1,0:T(8,128)(2,1)S(1)} %get-tuple-element.408, s32[]{:T(128)S(6)} %select_n.256), kind=kOutput, calls=%fused_computation.2.clone.1 | convolution fusion | flops 137361408 | bytes 4857860 | tf_op jit(solution)/shard_map/while/body/eval_jaxpr/qhgd,khd->hgqk/dot_general | solution.py:58
  87.8 0.0 copy-start
  87.8 3.7 %fusion.65 = f32[1,4,512,64]{2,3,1,0:T(8,128)S(1)} fusion(f32[512,512,4]{1,0,2:T(8,128)} %get-tuple-element.374, f32[4,512]{1,0:T(4,128)S(1)} %bitcast.102, pred[512,512]{0,1:T(8,128)(4,1)S(1)} %broadcast_compare_fusion.3, f32[1,4,512,64]{2,3,1,0:T(8,128)S(1)} %get-tuple-element.392, f32[4,512]{1,0:T(4,128)S(1)} %get-tuple-element.375, ...), kind=kOutput, calls=%fused_computation.9.clone.1 | convolution fusion | flops 139853824 | bytes 5652489 | tf_op jit(solution)/shard_map/while/body/eval_jaxpr/hgqk,khd->hgqd/dot_general | solution.py:67
  91.5 0.0 copy-done
  91.5 1.0 fusion.64
  92.6 0.1 select_reduce_fusion.3
  92.7 0.2 broadcast_compare_fusion.3
  93.0 2.7 %fusion.62 = (f32[4,512]{1,0:T(4,128)S(1)}, f32[512,512,4]{1,0,2:T(8,128)}) fusion(pred[512,512]{0,1:T(8,128)(4,1)S(1)} %broadcast_compare_fusion.3, bf16[512,1,4,64]{0,3,2,1:T(8,128)(2,1)S(1)} %get-tuple-element.409, bf16[2048,128]{1,0:T(8,128)(2,1)S(1)} %get-tuple-element.408, s32[]{:T(128)S(6)} %select_n.256), kind=kOutput, calls=%fused_computation.2.clone.1 | convolution fusion | flops 137361408 | bytes 4857860 | tf_op jit(solution)/shard_map/while/body/eval_jaxpr/qhgd,khd->hgqk/dot_general | solution.py:58
  95.7 0.0 copy-start
  95.7 3.7 %fusion.65 = f32[1,4,512,64]{2,3,1,0:T(8,128)S(1)} fusion(f32[512,512,4]{1,0,2:T(8,128)} %get-tuple-element.374, f32[4,512]{1,0:T(4,128)S(1)} %bitcast.102, pred[512,512]{0,1:T(8,128)(4,1)S(1)} %broadcast_compare_fusion.3, f32[1,4,512,64]{2,3,1,0:T(8,128)S(1)} %get-tuple-element.392, f32[4,512]{1,0:T(4,128)S(1)} %get-tuple-element.375, ...), kind=kOutput, calls=%fused_computation.9.clone.1 | convolution fusion | flops 139853824 | bytes 5652489 | tf_op jit(solution)/shard_map/while/body/eval_jaxpr/hgqk,khd->hgqd/dot_general | solution.py:67
  99.4 0.0 copy-done
  99.4 1.0 fusion.64
  100.5 0.1 fusion.35
  100.6 0.3 convert_element_type.42
  100.8 0.3 copy.22
  101.2 9.4 %all_to_all.21 = bf16[8,64,256]{2,1,0:T(8,128)(2,1)S(1)} all-to-all(bf16[8,64,256]{2,1,0:T(8,128)(2,1)S(1)} %copy.22), channel_id=1, replica_groups=mesh['grp'=4,'sp'=8] {'sp'}, dimensions={0} | all-to-all | bytes 524288 | tf_op jit(solution)/shard_map/all_to_all | solution.py:129
  110.6 0.7 copy.28
  (31 shorter events, 0.5 us)
Async XLA Ops:
  6.5 37.1 %all-gather.2.cloned.1.call-start = ((), (), s32[]{:S(2)}) async-start(), calls=%async_computation.2 | async-start | bytes 3391488 | tf_op jit(solution)/shard_map/all_gather | solution.py:95
  43.6 10.0 %copy-start.2 = (f32[32]{0:T(128)S(1)}, f32[32]{0:T(128)}, u32[]{:S(2)}) copy-start(f32[32]{0:T(128)} %param.11) | copy-start | bytes 388
  47.7 21.1 %copy-start.1 = (s32[16]{0:T(128)S(1)}, s32[16]{0:T(128)}, u32[]{:S(2)}) copy-start(s32[16]{0:T(128)} %param.10) | copy-start | bytes 196
  49.0 19.5 %all-to-all-start = ((bf16[4,512,128]{1,2,0:T(8,128)(2,1)}), bf16[4,512,128]{1,2,0:T(8,128)(2,1)S(1)}, u32[]{:S(2)}, u32[]{:S(2)}) async-start(bf16[4,512,128]{1,2,0:T(8,128)(2,1)} %stack.2), calls=%async_computation | async-start | bytes 1048576 | tf_op jit(solution)/shard_map/all_to_all | solution.py:113
  71.9 3.7 %copy-start = (f32[512,512,4]{1,0,2:T(8,128)S(1)}, f32[512,512,4]{1,0,2:T(8,128)}, u32[]{:S(2)}) copy-start(f32[512,512,4]{1,0,2:T(8,128)} %get-tuple-element.374) | copy-start | bytes 12582916 | tf_op jit(solution)/shard_map/while
  79.9 3.7 %copy-start = (f32[512,512,4]{1,0,2:T(8,128)S(1)}, f32[512,512,4]{1,0,2:T(8,128)}, u32[]{:S(2)}) copy-start(f32[512,512,4]{1,0,2:T(8,128)} %get-tuple-element.374) | copy-start | bytes 12582916 | tf_op jit(solution)/shard_map/while
  87.8 3.7 %copy-start = (f32[512,512,4]{1,0,2:T(8,128)S(1)}, f32[512,512,4]{1,0,2:T(8,128)}, u32[]{:S(2)}) copy-start(f32[512,512,4]{1,0,2:T(8,128)} %get-tuple-element.374) | copy-start | bytes 12582916 | tf_op jit(solution)/shard_map/while
  95.7 3.7 %copy-start = (f32[512,512,4]{1,0,2:T(8,128)S(1)}, f32[512,512,4]{1,0,2:T(8,128)}, u32[]{:S(2)}) copy-start(f32[512,512,4]{1,0,2:T(8,128)} %get-tuple-element.374) | copy-start | bytes 12582916 | tf_op jit(solution)/shard_map/while
Sparse Core Ops, SparseCore 0:
  9.2 34.3 all-gather.1
